TPU v7x, 32 devices: a whole 2x2x4 slice. The times are simulated.
32 devices in a mesh: gx: 4 (over z), gy: 2 (over core), gz: 4 (over y, x).
Axes of the slice: x: 2, y: 2, z: 4, core: 2. Of those that a mesh axis runs over, the one named last changes fastest.
Arguments:
- pair: bfloat16 [128, 512, 512], P('gz', 'gx', 'gy'), may hold values from -6 to 6
- pair_mask: int32 [512, 512], P('gx', 'gy'), may hold values from 0 to 1, as said below
- input_gain: float32 [128], replicated, may hold values from 0.1 to 1.9
- input_weights: bfloat16 [4, 128, 128], replicated, may hold values from -0.5 to 0.5
- out_gate_weight: bfloat16 [128, 128], replicated, may hold values from -0.5 to 0.5
- hidden_gain: float32 [128], replicated, may hold values from 0.1 to 1.9
- out_weight: bfloat16 [128, 128], replicated, may hold values from -0.5 to 0.5
Outputs:
- update: bfloat16 [128, 512, 512], P('gz', 'gx', 'gy')
Inputs may be any that keep to these rules, and one draw needn't show every extreme that they name: pair_mask[r, s] = m[r] * m[s] for a 0/1 residue mask m of the draw that is 0 for all r >= L, for one crop length L with 256 < L <= 512; residues below L may also be 0.
All inputs are finite; a program needn't handle non-finite values.
Results may differ from a plain program's by a relative error of at most 0.011.
Values may be sent and summed in bfloat16 or wider, within the bound.
A program may use at most 64 MiB of HBM per device.

v0:
```python
import functools

import jax
import jax.numpy as jnp
from jax import lax
from jax.experimental import pallas as pl
from jax.experimental.pallas import tpu as pltpu
from jax.sharding import PartitionSpec as P

EPSILON = 1e-05
MESH = pl.DeviceIdType.MESH


def position(axes):
    at = 0
    for name in axes:
        at = at * lax.axis_size(name) + lax.axis_index(name)
    return at


def coordinates(axes, at):
    where = {}
    for name in reversed(axes):
        where[name] = lax.rem(at, lax.axis_size(name))
        at = at // lax.axis_size(name)
    return where


ROWS = 8
LANES = 128


def panels(span):
    return [(at, slice(at * LANES, (at + 1) * LANES)) for at in range(span // LANES)]


def row_of(store, row, height, span):
    parts = [store[at, pl.ds(row, height, stride=ROWS), :] for at, _ in panels(span)]
    return jnp.concatenate(parts, axis=1)


def put_row(store, row, height, span, value):
    for at, lanes in panels(span):
        store[at, pl.ds(row, height, stride=ROWS), :] = value[:, lanes]


def pack(store, target, span):
    for at, lanes in panels(span):
        height = store.shape[1] // ROWS
        target[:, :, lanes] = store[at].reshape(height, ROWS, LANES).astype(jnp.bfloat16)


def greet(groups):
    barrier = pltpu.get_barrier_semaphore()
    total = 0
    for axes, count in groups:
        me = position(axes)

        @pl.loop(1, count)
        def _(step):
            there = coordinates(axes, lax.rem(me + step, count))
            pl.semaphore_signal(barrier, inc=1, device_id=there, device_id_type=MESH)

        total += count - 1
    pl.semaphore_wait(barrier, total)


def standardize(source, plain):
    values = source.astype(jnp.float32)
    average = jnp.sum(values, axis=0) / values.shape[0]
    centred = values - average
    spread = jnp.sum(centred * centred, axis=0) / values.shape[0]
    result = centred * lax.rsqrt(spread + EPSILON)
    for at, lanes in panels(values.shape[2]):
        plain[at] = result[:, :, lanes].reshape(plain.shape[1:])


def whole_kernel(
    flat, count, quads, pair, mask, input_gain, input_weights, out_gate_weight, hidden_gain, out_weight,
    update,
    turned, spread_gain, wide_left, far_right, gate, triangle,
    landed, plain, sided, outgoing, returned, finished,
    pair_send, pair_recv, pair_own, sends, receives, gsend, greceive, own,
    back_send, back_recv, out_send, out_recv, out_own,
):
    me = position(flat)
    quad = lax.axis_index("gz")
    core = lax.axis_index("gy")
    cores = lax.axis_size("gy")
    chunks, channels, _, span = landed.shape
    local = pair.shape[0]
    rows = chunks * ROWS
    hidden = outgoing.shape[2]
    channels = landed.shape[1]
    depth = hidden // count
    greet(((flat, count), (("gy",), cores)))

    def wide_gain(at):
        return jnp.concatenate([spread_gain[at]] * (span // LANES), axis=1)

    def inside_of(chunk, row):
        first = quad * rows + chunk * ROWS + row
        return mask[pl.ds(first, 1), :].astype(jnp.float32)

    columns = pl.ds(pl.multiple_of(core * span, span), span)

    def pair_copy(chunk, step, sender, target):
        first = pl.multiple_of(target * rows + chunk * ROWS, ROWS)
        return pltpu.make_async_remote_copy(
            src_ref=pair.at[:, pl.ds(first, ROWS), :],
            dst_ref=landed.at[chunk, pl.ds(sender * local, local)],
            send_sem=pair_send.at[chunk, step],
            recv_sem=pair_recv.at[chunk, step],
            device_id={"gz": target},
            device_id_type=MESH,
        )

    def pair_keep(chunk):
        first = pl.multiple_of(quad * rows + chunk * ROWS, ROWS)
        return pltpu.make_async_copy(
            pair.at[:, pl.ds(first, ROWS), :],
            landed.at[chunk, pl.ds(quad * local, local)],
            pair_own.at[chunk],
        )

    def landing(side, chunk, sender):
        cut = pl.ds(pl.multiple_of(chunk * ROWS, ROWS), ROWS)
        if side == 0:
            return wide_left.at[:, sender, cut, columns]
        return far_right.at[:, sender, cut, :]

    def copy(side, chunk, step, sender, target):
        return pltpu.make_async_remote_copy(
            src_ref=outgoing.at[side, chunk, pl.ds(target * depth, depth)],
            dst_ref=landing(side, chunk, sender),
            send_sem=sends.at[side, chunk, step],
            recv_sem=receives.at[side, chunk, step],
            device_id=coordinates(flat, target),
            device_id_type=MESH,
        )

    def keep(side, chunk):
        return pltpu.make_async_copy(
            outgoing.at[side, chunk, pl.ds(me * depth, depth)],
            landing(side, chunk, me),
            own.at[side, chunk],
        )

    def passed(chunk, ahead):
        cut = pl.ds(pl.multiple_of(chunk * ROWS, ROWS), ROWS)
        return pltpu.make_async_remote_copy(
            src_ref=wide_left.at[:, :, cut, columns],
            dst_ref=wide_left.at[:, :, cut, columns],
            send_sem=gsend.at[chunk, ahead],
            recv_sem=greceive.at[chunk, ahead],
            device_id={"gy": lax.rem(core + ahead, cores)},
            device_id_type=MESH,
        )

    @pl.loop(0, chunks)
    def _(chunk):
        pair_keep(chunk).start()

        @pl.loop(1, quads)
        def _(step):
            pair_copy(chunk, step, quad, lax.rem(quad + step, quads)).start()

    for at in range(4):
        turned[at] = input_weights[at].astype(jnp.float32).T.astype(jnp.bfloat16)
    turned[4] = out_gate_weight[...].astype(jnp.float32).T.astype(jnp.bfloat16)
    turned[5] = out_weight[...].astype(jnp.float32).T.astype(jnp.bfloat16)
    spread_gain[0] = jnp.broadcast_to(input_gain[...], (LANES, channels)).T
    spread_gain[1] = jnp.broadcast_to(hidden_gain[...], (LANES, hidden)).T

    @pl.loop(0, chunks)
    def _(chunk):
        @pl.loop(1, quads)
        def _(step):
            pair_copy(
                chunk, step, lax.rem(quad - step + quads, quads), lax.rem(quad + step, quads)
            ).wait()

        pair_keep(chunk).wait()
        standardize(landed[chunk], plain)

        def normed_row(row):
            return (row_of(plain, row, channels, span) * wide_gain(0)).astype(jnp.bfloat16)

        def product(at, normed):
            return jnp.dot(turned[at], normed, preferred_element_type=jnp.float32)

        for side in range(2):
            @pl.loop(0, ROWS)
            def _(row):
                normed = normed_row(row)
                gating = inside_of(chunk, row) * jax.nn.sigmoid(product(2 * side, normed))
                put_row(sided.at[side], row, hidden, span, gating * product(2 * side + 1, normed))

            pack(sided.at[side], outgoing.at[side, chunk], span)

            @pl.loop(1, count)
            def _(step):
                copy(side, chunk, step, me, lax.rem(me + step, count)).start()

            keep(side, chunk).start()

        @pl.loop(0, ROWS)
        def _(row):
            gate[chunk * ROWS + row] = jax.nn.sigmoid(product(4, normed_row(row)))

    @pl.loop(0, chunks)
    def _(chunk):
        for side in range(2):
            @pl.loop(1, count)
            def _(step):
                copy(
                    side, chunk, step, lax.rem(me - step + count, count), lax.rem(me + step, count)
                ).wait()

            keep(side, chunk).wait()
            if side == 0:
                for ahead in range(1, cores):
                    passed(chunk, ahead).start()

    @pl.loop(0, chunks)
    def _(chunk):
        for ahead in range(1, cores):
            passed(chunk, ahead).wait()

    def back_copy(chunk, step, sender, target):
        return pltpu.make_async_remote_copy(
            src_ref=triangle.at[:, target, chunk],
            dst_ref=returned.at[chunk, pl.ds(sender * depth, depth)],
            send_sem=back_send.at[chunk, step],
            recv_sem=back_recv.at[chunk, step],
            device_id=coordinates(flat, target),
            device_id_type=MESH,
        )

    def out_copy(chunk, step, sender, target):
        first = pl.multiple_of(sender * rows + chunk * ROWS, ROWS)
        return pltpu.make_async_remote_copy(
            src_ref=finished.at[chunk, pl.ds(target * local, local)],
            dst_ref=update.at[:, pl.ds(first, ROWS), :],
            send_sem=out_send.at[chunk, step],
            recv_sem=out_recv.at[chunk, step],
            device_id={"gz": target},
            device_id_type=MESH,
        )

    def out_keep(chunk):
        first = pl.multiple_of(quad * rows + chunk * ROWS, ROWS)
        return pltpu.make_async_copy(
            finished.at[chunk, pl.ds(quad * local, local)],
            update.at[:, pl.ds(first, ROWS), :],
            out_own.at[chunk],
        )

    @pl.loop(0, depth)
    def _(at):
        product = lax.dot_general(
            wide_left[at].reshape(count * rows, -1),
            far_right[at].reshape(count * rows, -1), (((0,), (0,)), ((), ())),
            preferred_element_type=jnp.float32,
        )
        triangle[at] = product.reshape(count, chunks, ROWS, span).astype(jnp.bfloat16)

    @pl.loop(0, chunks)
    def _(chunk):
        @pl.loop(1, count)
        def _(step):
            back_copy(chunk, step, me, lax.rem(me + step, count)).start()

    @pl.loop(0, chunks)
    def _(chunk):
        @pl.loop(0, depth)
        def _(at):
            returned[chunk, me * depth + at] = triangle[at, me, chunk]

        @pl.loop(1, count)
        def _(step):
            back_copy(
                chunk, step, lax.rem(me - step + count, count), lax.rem(me + step, count)
            ).wait()

        standardize(returned[chunk], plain)

        @pl.loop(0, ROWS)
        def _(row):
            normed = (row_of(plain, row, hidden, span) * wide_gain(1)).astype(jnp.bfloat16)
            inside = inside_of(chunk, row)
            projected = jnp.dot(turned[5], normed, preferred_element_type=jnp.float32)
            gated = inside * gate[chunk * ROWS + row] * projected
            put_row(sided.at[0], row, channels, span, gated)

        pack(sided.at[0], finished.at[chunk], span)

        @pl.loop(1, quads)
        def _(step):
            out_copy(chunk, step, quad, lax.rem(quad + step, quads)).start()

        out_keep(chunk).start()

    @pl.loop(0, chunks)
    def _(chunk):
        @pl.loop(1, quads)
        def _(step):
            out_copy(
                chunk, step, lax.rem(quad - step + quads, quads), lax.rem(quad + step, quads)
            ).wait()

        out_keep(chunk).wait()


def shards(pair, pair_mask, input_gain, input_weights, out_gate_weight, hidden_gain, out_weight):
    flat = ("gx", "gz")
    quads = lax.axis_size("gz")
    count = lax.axis_size("gx") * quads
    cores = lax.axis_size("gy")
    local, tall, span = pair.shape
    rows = tall // quads
    chunks = rows // ROWS
    channels = input_gain.shape[0]
    hidden = hidden_gain.shape[0]
    depth = hidden // count
    near = pl.BlockSpec(memory_space=pltpu.VMEM)
    far = pl.BlockSpec(memory_space=pl.ANY)
    copies = pltpu.SemaphoreType.DMA
    tiles = span // LANES
    tallest = max(channels, hidden)
    return pl.pallas_call(
        functools.partial(whole_kernel, flat, count, quads),
        out_shape=jax.ShapeDtypeStruct(pair.shape, jnp.bfloat16),
        in_specs=[far] + [near] * 6,
        out_specs=far,
        scratch_shapes=[
            pltpu.VMEM((6, tallest, tallest), jnp.bfloat16),
            pltpu.VMEM((2, tallest, LANES), jnp.float32),
            pltpu.VMEM((depth, count, rows, span * cores), jnp.bfloat16),
            pltpu.VMEM((depth, count, rows, span), jnp.bfloat16),
            pltpu.VMEM((rows, channels, span), jnp.float32),
            pltpu.VMEM((depth, count, chunks, ROWS, span), jnp.bfloat16),
            pltpu.VMEM((chunks, channels, ROWS, span), jnp.bfloat16),
            pltpu.VMEM((tiles, tallest * ROWS, LANES), jnp.float32),
            pltpu.VMEM((2, tiles, tallest * ROWS, LANES), jnp.float32),
            pltpu.VMEM((2, chunks, hidden, ROWS, span), jnp.bfloat16),
            pltpu.VMEM((chunks, hidden, ROWS, span), jnp.bfloat16),
            pltpu.VMEM((chunks, channels, ROWS, span), jnp.bfloat16),
            copies((chunks, quads)),
            copies((chunks, quads)),
            copies((chunks,)),
            copies((2, chunks, count)),
            copies((2, chunks, count)),
            copies((chunks, cores)),
            copies((chunks, cores)),
            copies((2, chunks)),
            copies((chunks, count)),
            copies((chunks, count)),
            copies((chunks, quads)),
            copies((chunks, quads)),
            copies((chunks,)),
        ],
        compiler_params=pltpu.CompilerParams(
            collective_id=0, has_side_effects=True, vmem_limit_bytes=60 << 20
        ),
    )(
        pair,
        pair_mask,
        input_gain[None],
        input_weights,
        out_gate_weight,
        hidden_gain[None],
        out_weight,
    )


def solution(mesh):
    placed = (P("gz", "gx", "gy"), P("gx", "gy"), P(), P(), P(), P(), P())
    return jax.shard_map(
        shards, mesh=mesh, in_specs=placed, out_specs=P("gz", "gx", "gy"), check_vma=False
    )
```

profile of v0, /device:TPU:12, one launch (start us, length us, event | category | flops | bytes accessed | tf_op | source)
XLA Modules:
  0.0 174.5 jit_solution(10749553355866019031)
XLA Ops:
  0.0 171.3 %shard_map.73 = bf16[32,128,256]{2,1,0:T(8,128)(2,1)} custom-call(bf16[32,128,256]{2,1,0:T(8,128)(2,1)} %pair.1, s32[128,256]{1,0:T(8,128)} %mask.1, f32[1,128]{1,0:T(1,128)} %bitcast.2, bf16[4,128,128]{2,1,0:T(8,128)(2,1)} %input_weights.1, bf16[128,128]{1,0:T(8,128)(2,1)} %out_gate_weight.1, f32[1,128]{1,0:T(1,128)} %bitcast.3, bf16[128,128]{1,0:T(8,128)(2,1)} %out_weight.1), custom_call_target="tpu_custom_call" | custom-call | tf_op jit(solution)/shard_map/pallas_call | solution.py:331
  171.3 3.1 %copy.9 = bf16[32,128,256]{2,1,0:T(8,128)(2,1)} copy(bf16[32,128,256]{2,1,0:T(8,128)(2,1)} %shard_map.73) | data formatting | bytes 4194304
where the time goes:
time: 176 us; the launch traced here: 174 us
  Pallas kernels  171 us (97%)
  local copies, waits for them, and re-layouts  3.13 us (2%)
    pallas_call x1, Pallas kernels, shards(): pl.pallas_call(functools.partial(whole_kernel, flat, count, quads), out_s...  171 us

commit v1 on v0

--- a/solution.py
+++ b/solution.py
@@ -65,8 +65,7 @@
     pl.semaphore_wait(barrier, total)
 
 
-def standardize(source, plain):
-    values = source.astype(jnp.float32)
+def standardize(values, plain):
     average = jnp.sum(values, axis=0) / values.shape[0]
     centred = values - average
     spread = jnp.sum(centred * centred, axis=0) / values.shape[0]
@@ -75,14 +74,23 @@
         plain[at] = result[:, :, lanes].reshape(plain.shape[1:])
 
 
+def wrapped(at, step, count):
+    moved = at + step
+    return jnp.where(moved >= count, moved - count, moved)
+
+
 def whole_kernel(
-    flat, count, quads, pair, mask, input_gain, input_weights, out_gate_weight, hidden_gain, out_weight,
+    flat, count, quads, split, pair, far_mask, far_input_gain, far_input_weights, far_gate_weight, far_hidden_gain,
+    far_out_weight,
     update,
-    turned, spread_gain, wide_left, far_right, gate, triangle,
+    mask, input_gain, input_weights, out_gate_weight, hidden_gain, out_weight, fetched,
+    turned, spread_gain, wide_left, far_right, half_left, half_right, gate, triangle,
     landed, plain, sided, outgoing, returned, finished,
-    pair_send, pair_recv, pair_own, sends, receives, gsend, greceive, own,
+    pair_send, pair_recv, pair_own, sends, receives, half_sends, half_receives, gsend, greceive, own,
     back_send, back_recv, out_send, out_recv, out_own,
 ):
+    whole_depth, half_depth = split
+    depth = whole_depth + half_depth
     me = position(flat)
     quad = lax.axis_index("gz")
     core = lax.axis_index("gy")
@@ -91,9 +99,26 @@
     local = pair.shape[0]
     rows = chunks * ROWS
     hidden = outgoing.shape[2]
-    channels = landed.shape[1]
-    depth = hidden // count
+    members = count // 2
+    half = lax.div(me, members)
+    member = me - half * members
+    base = half * members
+
+    fetches = [
+        pltpu.make_async_copy(source, target, fetched.at[at])
+        for at, (source, target) in enumerate((
+            (far_input_weights, input_weights), (far_input_gain, input_gain), (far_mask, mask),
+            (far_gate_weight, out_gate_weight), (far_hidden_gain, hidden_gain), (far_out_weight, out_weight),
+        ))
+    ]
+    for fetch in fetches:
+        fetch.start()
+
     greet(((flat, count), (("gy",), cores)))
+
+    def chip(at):
+        across = lax.div(at, quads)
+        return {"gx": across, "gz": at - across * quads}
 
     def wide_gain(at):
         return jnp.concatenate([spread_gain[at]] * (span // LANES), axis=1)
@@ -123,39 +148,100 @@
             pair_own.at[chunk],
         )
 
+    def cut_of(chunk):
+        return pl.ds(pl.multiple_of(chunk * ROWS, ROWS), ROWS)
+
     def landing(side, chunk, sender):
-        cut = pl.ds(pl.multiple_of(chunk * ROWS, ROWS), ROWS)
         if side == 0:
-            return wide_left.at[:, sender, cut, columns]
-        return far_right.at[:, sender, cut, :]
+            return wide_left.at[:, sender, cut_of(chunk), columns]
+        return far_right.at[:, sender, cut_of(chunk), :]
+
+    def half_landing(side, chunk, sender):
+        if side == 0:
+            return half_left.at[:, sender, cut_of(chunk), columns]
+        return half_right.at[:, sender, cut_of(chunk), :]
 
     def copy(side, chunk, step, sender, target):
         return pltpu.make_async_remote_copy(
-            src_ref=outgoing.at[side, chunk, pl.ds(target * depth, depth)],
+            src_ref=outgoing.at[side, chunk, pl.ds(target * whole_depth, whole_depth)],
             dst_ref=landing(side, chunk, sender),
             send_sem=sends.at[side, chunk, step],
             recv_sem=receives.at[side, chunk, step],
-            device_id=coordinates(flat, target),
+            device_id=chip(target),
+            device_id_type=MESH,
+        )
+
+    def half_part(target):
+        return pl.ds(count * whole_depth + target * half_depth, half_depth)
+
+    def half_copy(side, chunk, step, sender, target):
+        return pltpu.make_async_remote_copy(
+            src_ref=outgoing.at[side, chunk, half_part(target)],
+            dst_ref=half_landing(side, chunk, sender),
+            send_sem=half_sends.at[side, chunk, step],
+            recv_sem=half_receives.at[side, chunk, step],
+            device_id=chip(base + target),
             device_id_type=MESH,
         )
 
     def keep(side, chunk):
         return pltpu.make_async_copy(
-            outgoing.at[side, chunk, pl.ds(me * depth, depth)],
+            outgoing.at[side, chunk, pl.ds(me * whole_depth, whole_depth)],
             landing(side, chunk, me),
-            own.at[side, chunk],
+            own.at[0, side, chunk],
+        )
+
+    def half_keep(side, chunk):
+        return pltpu.make_async_copy(
+            outgoing.at[side, chunk, half_part(member)],
+            half_landing(side, chunk, member),
+            own.at[1, side, chunk],
         )
 
     def passed(chunk, ahead):
-        cut = pl.ds(pl.multiple_of(chunk * ROWS, ROWS), ROWS)
-        return pltpu.make_async_remote_copy(
-            src_ref=wide_left.at[:, :, cut, columns],
-            dst_ref=wide_left.at[:, :, cut, columns],
-            send_sem=gsend.at[chunk, ahead],
-            recv_sem=greceive.at[chunk, ahead],
-            device_id={"gy": lax.rem(core + ahead, cores)},
-            device_id_type=MESH,
-        )
+        where = {"gy": lax.rem(core + ahead, cores)}
+        made = []
+        for at, (store, used) in enumerate(((wide_left, whole_depth), (half_left, half_depth))):
+            if used:
+                made.append(pltpu.make_async_remote_copy(
+                    src_ref=store.at[:, :, cut_of(chunk), columns],
+                    dst_ref=store.at[:, :, cut_of(chunk), columns],
+                    send_sem=gsend.at[at, chunk, ahead],
+                    recv_sem=greceive.at[at, chunk, ahead],
+                    device_id=where,
+                    device_id_type=MESH,
+                ))
+        return made
+
+    def send(side, chunk):
+        if whole_depth:
+            @pl.loop(1, count)
+            def _(step):
+                copy(side, chunk, step, me, wrapped(me, step, count)).start()
+
+            keep(side, chunk).start()
+        if half_depth:
+            @pl.loop(1, members)
+            def _(step):
+                half_copy(side, chunk, step, member, wrapped(member, step, members)).start()
+
+            half_keep(side, chunk).start()
+
+    def receive(side, chunk):
+        if whole_depth:
+            @pl.loop(1, count)
+            def _(step):
+                copy(side, chunk, step, wrapped(me, count - step, count), wrapped(me, step, count)).wait()
+
+            keep(side, chunk).wait()
+        if half_depth:
+            @pl.loop(1, members)
+            def _(step):
+                half_copy(
+                    side, chunk, step, wrapped(member, members - step, members), wrapped(member, step, members)
+                ).wait()
+
+            half_keep(side, chunk).wait()
 
     @pl.loop(0, chunks)
     def _(chunk):
@@ -163,8 +249,10 @@
 
         @pl.loop(1, quads)
         def _(step):
-            pair_copy(chunk, step, quad, lax.rem(quad + step, quads)).start()
-
+            pair_copy(chunk, step, quad, wrapped(quad, step, quads)).start()
+
+    for fetch in fetches:
+        fetch.wait()
     for at in range(4):
         turned[at] = input_weights[at].astype(jnp.float32).T.astype(jnp.bfloat16)
     turned[4] = out_gate_weight[...].astype(jnp.float32).T.astype(jnp.bfloat16)
@@ -176,12 +264,10 @@
     def _(chunk):
         @pl.loop(1, quads)
         def _(step):
-            pair_copy(
-                chunk, step, lax.rem(quad - step + quads, quads), lax.rem(quad + step, quads)
-            ).wait()
+            pair_copy(chunk, step, wrapped(quad, quads - step, quads), wrapped(quad, step, quads)).wait()
 
         pair_keep(chunk).wait()
-        standardize(landed[chunk], plain)
+        standardize(landed[chunk].astype(jnp.float32), plain)
 
         def normed_row(row):
             return (row_of(plain, row, channels, span) * wide_gain(0)).astype(jnp.bfloat16)
@@ -197,12 +283,7 @@
                 put_row(sided.at[side], row, hidden, span, gating * product(2 * side + 1, normed))
 
             pack(sided.at[side], outgoing.at[side, chunk], span)
-
-            @pl.loop(1, count)
-            def _(step):
-                copy(side, chunk, step, me, lax.rem(me + step, count)).start()
-
-            keep(side, chunk).start()
+            send(side, chunk)
 
         @pl.loop(0, ROWS)
         def _(row):
@@ -211,29 +292,25 @@
     @pl.loop(0, chunks)
     def _(chunk):
         for side in range(2):
-            @pl.loop(1, count)
-            def _(step):
-                copy(
-                    side, chunk, step, lax.rem(me - step + count, count), lax.rem(me + step, count)
-                ).wait()
-
-            keep(side, chunk).wait()
+            receive(side, chunk)
             if side == 0:
                 for ahead in range(1, cores):
-                    passed(chunk, ahead).start()
+                    for made in passed(chunk, ahead):
+                        made.start()
 
     @pl.loop(0, chunks)
     def _(chunk):
         for ahead in range(1, cores):
-            passed(chunk, ahead).wait()
+            for made in passed(chunk, ahead):
+                made.wait()
 
     def back_copy(chunk, step, sender, target):
         return pltpu.make_async_remote_copy(
             src_ref=triangle.at[:, target, chunk],
-            dst_ref=returned.at[chunk, pl.ds(sender * depth, depth)],
+            dst_ref=returned.at[chunk, sender],
             send_sem=back_send.at[chunk, step],
             recv_sem=back_recv.at[chunk, step],
-            device_id=coordinates(flat, target),
+            device_id=chip(target),
             device_id_type=MESH,
         )
 
@@ -256,34 +333,49 @@
             out_own.at[chunk],
         )
 
-    @pl.loop(0, depth)
-    def _(at):
+    def multiply(left, right):
         product = lax.dot_general(
-            wide_left[at].reshape(count * rows, -1),
-            far_right[at].reshape(count * rows, -1), (((0,), (0,)), ((), ())),
-            preferred_element_type=jnp.float32,
-        )
-        triangle[at] = product.reshape(count, chunks, ROWS, span).astype(jnp.bfloat16)
+            left.reshape(left.shape[0] * rows, -1), right.reshape(right.shape[0] * rows, -1),
+            (((0,), (0,)), ((), ())), preferred_element_type=jnp.float32,
+        )
+        return product.reshape(count, chunks, ROWS, span).astype(jnp.bfloat16)
+
+    if whole_depth:
+        @pl.loop(0, whole_depth)
+        def _(at):
+            triangle[at] = multiply(wide_left[at], far_right[at])
+    if half_depth:
+        @pl.loop(0, half_depth)
+        def _(at):
+            triangle[whole_depth + at] = multiply(half_left[at], half_right[at])
 
     @pl.loop(0, chunks)
     def _(chunk):
         @pl.loop(1, count)
         def _(step):
-            back_copy(chunk, step, me, lax.rem(me + step, count)).start()
+            back_copy(chunk, step, me, wrapped(me, step, count)).start()
+
+    def gathered(chunk):
+        parts = []
+        if whole_depth:
+            parts.append(returned[chunk, :, :whole_depth].astype(jnp.float32).reshape(-1, ROWS, span))
+        if half_depth:
+            near = returned[chunk, :members, whole_depth:].astype(jnp.float32)
+            other = returned[chunk, members:, whole_depth:].astype(jnp.float32)
+            parts.append((near + other).reshape(-1, ROWS, span))
+        return jnp.concatenate(parts, axis=0) if len(parts) > 1 else parts[0]
 
     @pl.loop(0, chunks)
     def _(chunk):
         @pl.loop(0, depth)
         def _(at):
-            returned[chunk, me * depth + at] = triangle[at, me, chunk]
+            returned[chunk, me, at] = triangle[at, me, chunk]
 
         @pl.loop(1, count)
         def _(step):
-            back_copy(
-                chunk, step, lax.rem(me - step + count, count), lax.rem(me + step, count)
-            ).wait()
-
-        standardize(returned[chunk], plain)
+            back_copy(chunk, step, wrapped(me, count - step, count), wrapped(me, step, count)).wait()
+
+        standardize(gathered(chunk), plain)
 
         @pl.loop(0, ROWS)
         def _(row):
@@ -297,7 +389,7 @@
 
         @pl.loop(1, quads)
         def _(step):
-            out_copy(chunk, step, quad, lax.rem(quad + step, quads)).start()
+            out_copy(chunk, step, quad, wrapped(quad, step, quads)).start()
 
         out_keep(chunk).start()
 
@@ -305,9 +397,7 @@
     def _(chunk):
         @pl.loop(1, quads)
         def _(step):
-            out_copy(
-                chunk, step, lax.rem(quad - step + quads, quads), lax.rem(quad + step, quads)
-            ).wait()
+            out_copy(chunk, step, wrapped(quad, quads - step, quads), wrapped(quad, step, quads)).wait()
 
         out_keep(chunk).wait()
 
@@ -315,45 +405,57 @@
 def shards(pair, pair_mask, input_gain, input_weights, out_gate_weight, hidden_gain, out_weight):
     flat = ("gx", "gz")
     quads = lax.axis_size("gz")
-    count = lax.axis_size("gx") * quads
+    layers = lax.axis_size("gx")
+    count = layers * quads
     cores = lax.axis_size("gy")
     local, tall, span = pair.shape
     rows = tall // quads
     chunks = rows // ROWS
     channels = input_gain.shape[0]
     hidden = hidden_gain.shape[0]
-    depth = hidden // count
-    near = pl.BlockSpec(memory_space=pltpu.VMEM)
+    half_depth = 2 * (3 * (hidden // count) // 8) if layers % 2 == 0 else 0
+    members = count // 2
+    whole_depth = (hidden - half_depth * members) // count
+    depth = whole_depth + half_depth
+    stay = pl.BlockSpec(memory_space=pltpu.HBM)
     far = pl.BlockSpec(memory_space=pl.ANY)
     copies = pltpu.SemaphoreType.DMA
     tiles = span // LANES
     tallest = max(channels, hidden)
+    operands = (
+        pair_mask, input_gain[None], input_weights, out_gate_weight, hidden_gain[None], out_weight,
+    )
     return pl.pallas_call(
-        functools.partial(whole_kernel, flat, count, quads),
+        functools.partial(whole_kernel, flat, count, quads, (whole_depth, half_depth)),
         out_shape=jax.ShapeDtypeStruct(pair.shape, jnp.bfloat16),
-        in_specs=[far] + [near] * 6,
+        in_specs=[stay] * 7,
         out_specs=far,
-        scratch_shapes=[
+        scratch_shapes=[pltpu.VMEM(one.shape, one.dtype) for one in operands] + [
+            copies((len(operands),)),
             pltpu.VMEM((6, tallest, tallest), jnp.bfloat16),
             pltpu.VMEM((2, tallest, LANES), jnp.float32),
-            pltpu.VMEM((depth, count, rows, span * cores), jnp.bfloat16),
-            pltpu.VMEM((depth, count, rows, span), jnp.bfloat16),
+            pltpu.VMEM((max(whole_depth, 1), count, rows, span * cores), jnp.bfloat16),
+            pltpu.VMEM((max(whole_depth, 1), count, rows, span), jnp.bfloat16),
+            pltpu.VMEM((max(half_depth, 1), members, rows, span * cores), jnp.bfloat16),
+            pltpu.VMEM((max(half_depth, 1), members, rows, span), jnp.bfloat16),
             pltpu.VMEM((rows, channels, span), jnp.float32),
             pltpu.VMEM((depth, count, chunks, ROWS, span), jnp.bfloat16),
             pltpu.VMEM((chunks, channels, ROWS, span), jnp.bfloat16),
             pltpu.VMEM((tiles, tallest * ROWS, LANES), jnp.float32),
             pltpu.VMEM((2, tiles, tallest * ROWS, LANES), jnp.float32),
             pltpu.VMEM((2, chunks, hidden, ROWS, span), jnp.bfloat16),
-            pltpu.VMEM((chunks, hidden, ROWS, span), jnp.bfloat16),
+            pltpu.VMEM((chunks, count, depth, ROWS, span), jnp.bfloat16),
             pltpu.VMEM((chunks, channels, ROWS, span), jnp.bfloat16),
             copies((chunks, quads)),
             copies((chunks, quads)),
             copies((chunks,)),
             copies((2, chunks, count)),
             copies((2, chunks, count)),
-            copies((chunks, cores)),
-            copies((chunks, cores)),
-            copies((2, chunks)),
+            copies((2, chunks, members)),
+            copies((2, chunks, members)),
+            copies((2, chunks, cores)),
+            copies((2, chunks, cores)),
+            copies((2, 2, chunks)),
             copies((chunks, count)),
             copies((chunks, count)),
             copies((chunks, quads)),
@@ -361,17 +463,9 @@
             copies((chunks,)),
         ],
         compiler_params=pltpu.CompilerParams(
-            collective_id=0, has_side_effects=True, vmem_limit_bytes=60 << 20
+            collective_id=0, has_side_effects=True, vmem_limit_bytes=40 << 20
         ),
-    )(
-        pair,
-        pair_mask,
-        input_gain[None],
-        input_weights,
-        out_gate_weight,
-        hidden_gain[None],
-        out_weight,
-    )
+    )(*[pltpu.with_memory_space_constraint(one, pltpu.HBM) for one in (pair, *operands)])
 
 
 def solution(mesh):

time: 176 us -> 158 us (0.90)
  Pallas kernels: 171 us -> 156 us
  local copies, waits for them, and re-layouts: 3.13 us -> 1.32 us
    pallas_call x1, Pallas kernels: 171 us -> 156 us  [shards(): pl.pallas_call(functools.partial(whole_kernel, flat, count, quads, (whole...]
    unnamed x1, local copies, waits for them, and re-layouts: 3.13 us -> 1.32 us
where the time goes in v1:
time: 158 us
  Pallas kernels  156 us (99%)
    pallas_call x1, Pallas kernels, shards(): pl.pallas_call(functools.partial(whole_kernel, flat, count, quads, (whole...  156 us

profile of v1, /device:TPU:12, one launch (start us, length us, event | category | flops | bytes accessed | tf_op | source)
XLA Modules:
  0.0 157.8 jit_solution(9187582444949162837)
XLA Ops:
  0.0 156.5 %shard_map.73 = bf16[32,128,256]{2,1,0:T(8,128)(2,1)S(1)} custom-call(bf16[32,128,256]{2,1,0:T(8,128)(2,1)} %pair.1, s32[128,256]{1,0:T(8,128)} %far_mask.1, f32[1,128]{1,0:T(1,128)} %bitcast.2, bf16[4,128,128]{2,1,0:T(8,128)(2,1)} %far_input_weights.1, bf16[128,128]{1,0:T(8,128)(2,1)} %far_gate_weight.1, f32[1,128]{1,0:T(1,128)} %bitcast.3, ...), custom_call_target="tpu_custom_call" | custom-call | tf_op jit(solution)/shard_map/pallas_call | solution.py:428
  156.5 1.3 copy.9
